TPU v7x, 16 devices: a 4x2x1 block of a 4x4x8 slice. The times are simulated.
16 devices in a mesh: dp: 2 (over y, z), tp: 8 (over x, core).
Axes of the slice: x: 4, y: 2, z: 1, core: 2. Of those that a mesh axis runs over, the one named last changes fastest.
The devices are a block of a 4x4x8 slice.
Arguments:
- token_ids: int32 [16384], P('dp'), parts along dimension 0
- embed_table: bfloat16 [151936, 896], P('tp')
- norm_gain: bfloat16 [896], replicated
- w_in: bfloat16 [896, 4864], P(None, 'tp')
- w_out: bfloat16 [4864, 896], P('tp')
Outputs:
- output: bfloat16 [16384, 896], P(('dp', 'tp')), parts along dimension 0
There are 2 independent parts. A program takes and returns all parts, laid end to end along the dimension named above; an argument that names none is the same for every part.
All inputs are finite; a program needn't handle non-finite values.
Results may differ from a plain program's by a relative error of at most 0.0079017.
Values are sent between devices in bfloat16 or wider.
A program may use at most 768 MiB of HBM per device.

v0:
```python
import jax
import jax.numpy as jnp
from jax import lax
from jax.sharding import PartitionSpec as P

RMS_EPS = 1e-6


def rms_norm(row_vals, norm_gain):
    rows_f32 = row_vals.astype(jnp.float32)
    inv_rms = lax.rsqrt(jnp.mean(rows_f32 * rows_f32, axis=-1, keepdims=True) + RMS_EPS)
    return (rows_f32 * inv_rms * norm_gain.astype(jnp.float32)).astype(jnp.bfloat16)


def solution(mesh):
    def device_step(token_ids, table_shard, norm_gain, w_in_shard, w_out_shard):
        shard_rows = table_shard.shape[0]
        row_offset = lax.axis_index("tp") * shard_rows
        local_ids = token_ids - row_offset
        owned = (local_ids >= 0) & (local_ids < shard_rows)
        looked_up = jnp.take(table_shard, jnp.clip(local_ids, 0, shard_rows - 1), axis=0, mode="clip")
        partial_rows = jnp.where(owned[:, None], looked_up, jnp.zeros((), jnp.bfloat16))
        embedded = lax.psum_scatter(partial_rows, "tp", scatter_dimension=0, tiled=True)
        normed = rms_norm(embedded, norm_gain)
        normed_all = lax.all_gather(normed, "tp", axis=0, tiled=True)
        pre_act = jnp.dot(normed_all, w_in_shard, preferred_element_type=jnp.float32).astype(jnp.bfloat16)
        activated = jax.nn.gelu(pre_act.astype(jnp.float32), approximate=True).astype(jnp.bfloat16)
        mlp_part = jnp.dot(activated, w_out_shard, preferred_element_type=jnp.float32)
        mlp_sum = lax.psum_scatter(mlp_part, "tp", scatter_dimension=0, tiled=True)
        return (embedded.astype(jnp.float32) + mlp_sum).astype(jnp.bfloat16)

    return jax.shard_map(
        device_step,
        mesh=mesh,
        in_specs=(P("dp"), P("tp", None), P(), P(None, "tp"), P("tp", None)),
        out_specs=P(("dp", "tp"), None),
        check_vma=False,
    )
```

profile of v0, /device:TPU:112, one launch (start us, length us, event | category | flops | bytes accessed | tf_op | source)
XLA Modules:
  0.0 751.4 jit_solution(5032081025645221131)
XLA Ops:
  6.5 0.0 copy-start
  6.6 0.0 reduce-scatter.3.cloned.1.call-start
  6.6 0.9 compare_and_fusion
  7.4 0.8 clamp_clamp_fusion
  8.2 310.1 %gather_fusion = bf16[8192,896]{1,0:T(8,128)(2,1)} fusion(bf16[18992,896]{1,0:T(8,128)(2,1)} %param.6, s32[8192]{0:T(1024)S(1)} %clamp_clamp_fusion), kind=kCustom, calls=%fused_computation | custom fusion | bytes 29392896 | tf_op jit(solution)/shard_map/jit(_take)/gather | solution.py:21
  318.3 14.7 %broadcast_select_fusion = bf16[8192,896]{1,0:T(8,128)(2,1)} fusion(bf16[8192,896]{1,0:T(8,128)(2,1)} %gather_fusion, pred[8192]{0:T(1024)(128)(4,1)S(1)} %compare_and_fusion), kind=kLoop, calls=%fused_computation.11 | loop fusion | flops 7340032 | bytes 29368320 | tf_op jit(solution)/shard_map/jit(_where)/select_n | solution.py:22
  333.0 0.0 copy-start.3
  333.0 0.0 copy-start.4
  333.0 0.1 reduce-scatter.3.cloned.1.call-update
  333.1 0.1 all-gather.2.cloned.1.call-start
  333.1 0.5 copy-done.3
  333.7 153.5 %reduce-scatter.3.cloned.1.call-done = bf16[1024,896]{1,0:T(8,128)(2,1)} async-done(((bf16[8192,896]{1,0:T(8,128)(2,1)}), bf16[1024,896]{1,0:T(8,128)(2,1)}) %reduce-scatter.3.cloned.1.call-update) | async-done | bytes 1835024 | tf_op jit(solution)/shard_map/reduce_scatter | solution.py:23
  487.2 1.9 fusion.12
  489.1 3.2 fusion.14
  492.3 0.1 all-gather.2.cloned.1.call-update
  492.4 0.1 reduce-scatter.5.cloned.1.call-start
  492.5 72.0 %all-gather.2.cloned.1.call-done = bf16[8192,896]{1,0:T(8,128)(2,1)} async-done(((bf16[1024,896]{1,0:T(8,128)(2,1)}), bf16[8192,896]{1,0:T(8,128)(2,1)}) %all-gather.2.cloned.1.call-update) | async-done | bytes 14680080 | tf_op jit(solution)/shard_map/all_gather | solution.py:25
  564.4 0.0 copy-done
  564.4 0.0 copy-done.4
  564.4 28.8 %fusion.6 = f32[8192,896]{1,0:T(8,128)} fusion(bf16[608,896]{1,0:T(8,128)(2,1)S(1)} %copy-done, bf16[8192,896]{1,0:T(8,128)(2,1)} %all-gather.2.cloned.1.call-done, bf16[896,608]{0,1:T(8,128)(2,1)S(1)} %copy-done.4), kind=kOutput, calls=%fused_computation.13 | convolution fusion | flops 17905745920 | bytes 46219264 | tf_op jit(solution)/shard_map/dot_general | solution.py:28
  593.3 0.0 copy-start.1
  593.3 0.0 copy-start.2
  593.3 0.1 reduce-scatter.5.cloned.1.call-update
  593.3 147.8 %reduce-scatter.5.cloned.1.call-done = f32[1024,896]{1,0:T(8,128)} async-done(((f32[8192,896]{1,0:T(8,128)}), f32[1024,896]{1,0:T(8,128)}) %reduce-scatter.5.cloned.1.call-update) | async-done | bytes 3670032 | tf_op jit(solution)/shard_map/reduce_scatter | solution.py:29
  741.1 0.0 copy-done.2
  741.1 3.7 fusion.15
  744.8 0.0 copy-done.1
  (2 shorter events, 0.0 us)
Async XLA Ops:
  6.5 557.9 %copy-start = (bf16[608,896]{1,0:T(8,128)(2,1)S(1)}, bf16[608,896]{1,0:T(8,128)(2,1)}, u32[]{:S(2)}) copy-start(bf16[608,896]{1,0:T(8,128)(2,1)} %param.9) | copy-start | bytes 3268612
  6.6 480.6 %reduce-scatter.3.cloned.1.call-start = ((), (), s32[]{:S(2)}) async-start(), calls=%async_computation.2 | async-start | bytes 16515072 | tf_op jit(solution)/shard_map/reduce_scatter | solution.py:23
  333.0 0.7 copy-start.3
  333.0 231.4 %copy-start.4 = (bf16[896,608]{0,1:T(8,128)(2,1)S(1)}, bf16[896,608]{0,1:T(8,128)(2,1)}, u32[]{:S(2)}) copy-start(bf16[896,608]{0,1:T(8,128)(2,1)} %param.8) | copy-start | bytes 3268612
  333.1 231.3 %all-gather.2.cloned.1.call-start = ((), (), s32[]{:S(2)}) async-start(), calls=%async_computation.3 | async-start | bytes 16515072 | tf_op jit(solution)/shard_map/all_gather | solution.py:25
  492.4 248.7 %reduce-scatter.5.cloned.1.call-start = ((), (), s32[]{:S(2)}) async-start(), calls=%async_computation.4 | async-start | bytes 33030144 | tf_op jit(solution)/shard_map/reduce_scatter | solution.py:29
  593.3 151.6 %copy-start.1 = (bf16[608,896]{1,0:T(8,128)(2,1)S(1)}, bf16[608,896]{1,0:T(8,128)(2,1)}, u32[]{:S(2)}) copy-start(bf16[608,896]{1,0:T(8,128)(2,1)} %param.9) | copy-start | bytes 3268612
  593.3 147.8 %copy-start.2 = (bf16[1024,896]{1,0:T(8,128)(2,1)S(1)}, bf16[1024,896]{1,0:T(8,128)(2,1)}, u32[]{:S(2)}) copy-start(bf16[1024,896]{1,0:T(8,128)(2,1)} %reduce-scatter.3.cloned.1.call-done) | copy-start | bytes 5505028
Sparse Core Ops, SparseCore 0:
  333.2 153.9 reduce-scatter.2
  492.5 71.8 all-gather.1
  593.4 147.5 reduce-scatter.4
where the time goes:
time: 756 us; the launch traced here: 751 us
  waiting for transfers between devices  373 us (49%)
  local copies, waits for them, and re-layouts  311 us (41%)
  matrix products  28.8 us (4%)
  other arithmetic  25.3 us (3%)
  between operations  13.2 us (2%)
    gather x1, local copies, waits for them, and re-layouts, device_step(): jnp.take(table_shard, jnp.clip(local_ids, 0, shard_rows - 1), axis=0, mod...  310 us
    reduce_scatter x1, waiting for transfers between devices, device_step(): lax.psum_scatter(partial_rows, 'tp', scatter_dimension=0, tiled=True)  153 us
    reduce_scatter x1, waiting for transfers between devices, device_step(): mlp_sum = lax.psum_scatter(mlp_part, 'tp', scatter_dimension=0, tiled=True)  148 us
    all_gather x1, waiting for transfers between devices, device_step(): normed_all = lax.all_gather(normed, 'tp', axis=0, tiled=True)  72 us
    dot_general x1, matrix products, device_step(): jnp.dot(activated, w_out_shard, preferred_element_type=jnp.float32)  28.8 us
  transfers between devices with their start and end apart: 3, of which 3 were waited for; matrix products, arithmetic and copies ran while one was open for 0% of the time, Pallas kernels for 0%

commit v1 on v0

v1 whole, which is shorter than its diff:
```python
import functools

import jax
import jax.numpy as jnp
from jax import lax
from jax.experimental import pallas as pl
from jax.experimental.pallas import tpu as pltpu
from jax.sharding import PartitionSpec as P

RMS_EPS = 1e-6
MESH = pl.DeviceIdType.MESH
SUB = 8
GELU_C = 0.7978845608028654
MIB = 2**20


def pick_rows(rows, idx_ref, base):
    width = rows.shape[-1]
    iota = lax.broadcasted_iota(jnp.int32, (SUB, width), 0)
    acc = jnp.zeros((SUB, width), jnp.float32)
    for p in range(SUB):
        idx = idx_ref[base + p]
        row = jnp.maximum(idx, 0)
        tile = rows[lax.shift_right_logical(row, 3)].astype(jnp.float32)
        tile = pltpu.roll(tile, (p + SUB - (row & 7)) & 7, 0)
        acc = jnp.where(iota == jnp.where(idx >= 0, p, SUB), tile, acc)
    return acc


def gather_kernel(chunks, groups, idx_ref, table_hbm, out_ref, table, sem):
    step = pl.program_id(0)
    tiles = table.shape[0]

    @pl.when(step == 0)
    def _():
        copies = []
        for i in range(chunks):
            lo, hi = tiles * i // chunks, tiles * (i + 1) // chunks
            part = pl.ds(lo, hi - lo)
            copies.append(pltpu.make_async_copy(table_hbm.at[part], table.at[part], sem.at[i]))
        for copy in copies:
            copy.start()
        for copy in copies:
            copy.wait()

    def body(group, carry):
        out_ref[group] = pick_rows(table, idx_ref, (step * groups + group) * SUB).astype(jnp.bfloat16)
        return carry

    lax.fori_loop(0, groups, body, 0, unroll=2)


def gather_rows(idx, table, groups=64):
    width = table.shape[1]
    table3 = table.reshape(table.shape[0] // SUB, SUB, width)
    count = idx.shape[0] // SUB
    chunks = 8
    return pl.pallas_call(
        functools.partial(gather_kernel, chunks, groups),
        out_shape=jax.ShapeDtypeStruct((count, SUB, width), jnp.bfloat16),
        grid_spec=pltpu.PrefetchScalarGridSpec(
            num_scalar_prefetch=1,
            grid=(count // groups,),
            in_specs=[pl.BlockSpec(memory_space=pl.ANY)],
            out_specs=pl.BlockSpec((groups, SUB, width), lambda i, _: (i, 0, 0)),
            scratch_shapes=[pltpu.VMEM(table3.shape, jnp.bfloat16), pltpu.SemaphoreType.DMA((chunks,))],
        ),
        compiler_params=pltpu.CompilerParams(vmem_limit_bytes=48 * MIB),
    )(idx, table3)


def block_kernel(chips, ridx, sent_hbm, gain_ref, w1_hbm, w2_hbm, out_ref,
                 own, sib_part, got, fwd_up, fwd_dn, w1, w2, x_ref, n_ref, y_ref,
                 loc_sem, d2d_s, d2d_r, row_s, row_r, wx_s, wx_r, wy_s, wy_r, wd_s, wd_r):
    dp, tp = lax.axis_index("dp"), lax.axis_index("tp")
    chip, core = tp // 2, lax.rem(tp, 2)
    half = lax.rem(dp, 2)
    other = 1 - core
    sib = {"tp": chip * 2 + other}
    up = {"tp": lax.rem(chip + 1, chips) * 2 + core}
    dn = {"tp": lax.rem(chip + chips - 1, chips) * 2 + core}
    pair = {"dp": dp + 1 - 2 * half}
    groups = own.shape[1]
    mid = groups // 2
    k_in, width = w1.shape[1], w2.shape[1]
    r1 = pl.ds(pl.multiple_of(half * (k_in // 2), k_in // 2), k_in // 2)
    r2 = pl.ds(pl.multiple_of(half * (width // 2), width // 2), width // 2)

    def rcopy(src, dst, ss, rs, dev):
        return pltpu.make_async_remote_copy(src_ref=src, dst_ref=dst, send_sem=ss, recv_sem=rs,
                                            device_id=dev, device_id_type=MESH)

    barrier = pltpu.get_barrier_semaphore()
    for dev in (sib, up, dn, pair):
        pl.semaphore_signal(barrier, inc=1, device_id=dev, device_id_type=MESH)
    pl.semaphore_wait(barrier, 4)

    def mine(j):
        return j * 2 + core

    def theirs(j):
        return j * 2 + other

    wx = {
        (1, 1): rcopy(w1_hbm.at[r1], w1.at[mine(1), r1], wx_s.at[0], wx_r.at[0], up),
        (3, 1): rcopy(w1_hbm.at[r1], w1.at[mine(3), r1], wx_s.at[1], wx_r.at[1], dn),
        (1, 2): rcopy(w2_hbm.at[r2], w2.at[mine(1), r2], wx_s.at[2], wx_r.at[2], up),
        (3, 2): rcopy(w2_hbm.at[r2], w2.at[mine(3), r2], wx_s.at[3], wx_r.at[3], dn),
        (2, 1): rcopy(w1.at[mine(1), r1], w1.at[mine(2), r1], wx_s.at[4], wx_r.at[4], up),
        (2, 2): rcopy(w2.at[mine(3), r2], w2.at[mine(2), r2], wx_s.at[5], wx_r.at[5], dn),
    }
    wy, wd = {}, {}
    for j in (1, 2, 3):
        wy[j, 1] = rcopy(w1.at[mine(j), r1], w1.at[mine(j), r1], wy_s.at[2 * j - 2], wy_r.at[2 * j - 2], pair)
        wy[j, 2] = rcopy(w2.at[mine(j), r2], w2.at[mine(j), r2], wy_s.at[2 * j - 1], wy_r.at[2 * j - 1], pair)
    for j in (0, 1, 2, 3):
        s1, s2 = (w1_hbm, w2_hbm) if j == 0 else (w1.at[mine(j)], w2.at[mine(j)])
        wd[j, 1] = rcopy(s1, w1.at[mine(j)], wd_s.at[2 * j], wd_r.at[2 * j], sib)
        wd[j, 2] = rcopy(s2, w2.at[mine(j)], wd_s.at[2 * j + 1], wd_r.at[2 * j + 1], sib)

    d2d, loc = {}, {}
    for j in range(4):
        dest = lax.rem(chip + j, chips) * 2
        d2d[j] = rcopy(sent_hbm.at[dest + other], sib_part.at[j], d2d_s.at[j], d2d_r.at[j], sib)
        loc[j] = pltpu.make_async_copy(sent_hbm.at[dest + core], own.at[j], loc_sem.at[j])
    w1_loc = pltpu.make_async_copy(w1_hbm, w1.at[mine(0)], loc_sem.at[4])
    w2_loc = pltpu.make_async_copy(w2_hbm, w2.at[mine(0)], loc_sem.at[5])

    lo, hi = pl.ds(0, mid), pl.ds(mid, groups - mid)

    def slot(j, part=None):
        if part is None:
            return got.at[pl.ds(j * groups, groups)]
        return got.at[pl.ds(j * groups + part * mid, mid)]

    rows = {
        "2u": rcopy(own.at[2, lo], fwd_up, row_s.at[0], row_r.at[0], up),
        "2d": rcopy(own.at[2, hi], fwd_dn, row_s.at[1], row_r.at[1], dn),
        "1": rcopy(own.at[1], slot(1), row_s.at[2], row_r.at[2], up),
        "3": rcopy(own.at[3], slot(3), row_s.at[3], row_r.at[3], dn),
        "fu": rcopy(fwd_up, slot(2, 0), row_s.at[4], row_r.at[4], up),
        "fd": rcopy(fwd_dn, slot(2, 1), row_s.at[5], row_r.at[5], dn),
    }

    for key in ((1, 1), (3, 1), (1, 2), (3, 2)):
        wx[key].start()
    for j in (2, 1, 3, 0):
        d2d[j].start()
        loc[j].start()
    wd[0, 1].start()
    wd[0, 2].start()
    w1_loc.start()
    w2_loc.start()

    batch = 4
    for j in (2, 1, 3, 0):
        d2d[j].wait_recv()
        loc[j].wait()

        def add(i, carry, j=j):
            part = pl.ds(i * batch, batch)
            total = own[j, part] + sib_part[j, part]
            if j == 0:
                got[part] = total
            else:
                own[j, part] = total
            return carry

        lax.fori_loop(0, groups // batch, add, 0)
        if j == 2:
            rows["2u"].start()
            rows["2d"].start()
        elif j:
            rows[str(j)].start()

    wx[1, 1].wait_recv()
    wx[2, 1].start()
    wy[1, 1].start()
    wx[3, 1].wait_recv()
    wy[3, 1].start()
    wx[3, 2].wait_recv()
    wx[2, 2].start()
    wy[3, 2].start()
    wx[1, 2].wait_recv()
    wy[1, 2].start()
    rows["2u"].wait_recv()
    rows["fu"].start()
    rows["2d"].wait_recv()
    rows["fd"].start()
    for j, m in ((1, 1), (3, 1), (3, 2), (1, 2)):
        wy[j, m].wait_recv()
        wd[j, m].start()
    wx[2, 1].wait_recv()
    wy[2, 1].start()
    wx[2, 2].wait_recv()
    wy[2, 2].start()
    for key in ("1", "3", "fu", "fd"):
        rows[key].wait_recv()

    gain = gain_ref[...].astype(jnp.float32)

    def take(i, carry):
        x = jnp.concatenate([pick_rows(got, ridx, i * 16), pick_rows(got, ridx, i * 16 + SUB)], axis=0)
        inv = lax.rsqrt(jnp.mean(x * x, axis=-1, keepdims=True) + RMS_EPS)
        at = pl.ds(pl.multiple_of(i * 16, 16), 16)
        x_ref[at, :] = x.astype(jnp.bfloat16)
        n_ref[at, :] = (x * inv * gain).astype(jnp.bfloat16)
        return carry

    tokens = out_ref.shape[0]
    lax.fori_loop(0, tokens // 16, take, 0)

    block = 256

    def mlp(s, first=False, last=False):
        def body(i, carry):
            at = pl.ds(pl.multiple_of(i * block, block), block)
            u = jnp.dot(n_ref[at, :], w1[s], preferred_element_type=jnp.float32)
            z = u.astype(jnp.bfloat16).astype(jnp.float32)
            h = 0.5 * z * (1.0 + jnp.tanh(GELU_C * (z + 0.044715 * (z * z * z))))
            y = jnp.dot(h.astype(jnp.bfloat16), w2[s], preferred_element_type=jnp.float32)
            if not first:
                y = y_ref[at, :] + y
            if last:
                out_ref[at, :] = (x_ref[at, :].astype(jnp.float32) + y).astype(jnp.bfloat16)
            else:
                y_ref[at, :] = y
            return carry

        lax.fori_loop(0, tokens // block, body, 0)

    w1_loc.wait()
    w2_loc.wait()
    mlp(mine(0), first=True)
    wd[0, 1].wait_recv()
    wd[0, 2].wait_recv()
    mlp(theirs(0))
    for m in (1, 2):
        wy[2, m].wait_recv()
        wd[2, m].start()
    for j in (1, 3, 2):
        mlp(mine(j))
        wd[j, 1].wait_recv()
        wd[j, 2].wait_recv()
        mlp(theirs(j), last=j == 2)

    for table in (wx, wy, wd, d2d, rows):
        for copy in table.values():
            copy.wait_send()


def solution(mesh):
    chips = mesh.shape["tp"] // 2

    def device_step(token_ids, table, norm_gain, w1, w2):
        shard_rows, width = table.shape
        ranks = mesh.shape["tp"]
        tokens = token_ids.shape[0] // ranks
        tp = lax.axis_index("tp")
        cap = tokens
        local = token_ids - tp * shard_rows
        send_idx = jnp.where((local >= 0) & (local < shard_rows), local, -1)
        ids_mine = lax.dynamic_slice(token_ids, (tp * tokens,), (tokens,))
        rel = (tp // 2 - ids_mine // (2 * shard_rows) + chips) % chips
        ridx = rel * cap + jnp.arange(tokens, dtype=jnp.int32)
        sent = gather_rows(send_idx, table).reshape(ranks, cap // SUB, SUB, width)
        groups = cap // SUB
        hidden = w1.shape[1]
        bf, f32 = jnp.bfloat16, jnp.float32
        dma = pltpu.SemaphoreType.DMA
        anyspec = pl.BlockSpec(memory_space=pl.ANY)
        return pl.pallas_call(
            functools.partial(block_kernel, chips),
            out_shape=jax.ShapeDtypeStruct((tokens, width), bf),
            in_specs=[
                pl.BlockSpec(memory_space=pltpu.SMEM),
                anyspec,
                pl.BlockSpec(memory_space=pltpu.VMEM),
                anyspec,
                anyspec,
            ],
            out_specs=pl.BlockSpec(memory_space=pltpu.VMEM),
            scratch_shapes=[
                pltpu.VMEM((4, groups, SUB, width), bf),
                pltpu.VMEM((4, groups, SUB, width), bf),
                pltpu.VMEM((4 * groups, SUB, width), bf),
                pltpu.VMEM((groups // 2, SUB, width), bf),
                pltpu.VMEM((groups // 2, SUB, width), bf),
                pltpu.VMEM((ranks, width, hidden), bf),
                pltpu.VMEM((ranks, hidden, width), bf),
                pltpu.VMEM((tokens, width), bf),
                pltpu.VMEM((tokens, width), bf),
                pltpu.VMEM((tokens, width), f32),
                dma((6,)),
                dma((4,)), dma((4,)),
                dma((6,)), dma((6,)),
                dma((6,)), dma((6,)),
                dma((6,)), dma((6,)),
                dma((8,)), dma((8,)),
            ],
            compiler_params=pltpu.CompilerParams(
                collective_id=0, has_side_effects=True, vmem_limit_bytes=67043328
            ),
        )(ridx, sent, norm_gain.reshape(1, width), w1, w2)

    return jax.shard_map(
        device_step,
        mesh=mesh,
        in_specs=(P("dp"), P("tp", None), P(), P(None, "tp"), P("tp", None)),
        out_specs=P(("dp", "tp"), None),
        check_vma=False,
    )
```

time: 756 us -> 227 us (0.30)
  waiting for transfers between devices: 373 us -> 0 us
  local copies, waits for them, and re-layouts: 311 us -> 6.5 us
  Pallas kernels: 0 us -> 218 us
  matrix products: 28.8 us -> 0 us
  other arithmetic: 25.3 us -> 2.06 us
  between operations: 13.2 us -> 0.02 us
    gather x1 -> x0, local copies, waits for them, and re-layouts: 310 us -> none  [device_step(): jnp.take(table_shard, jnp.clip(local_ids, 0, shard_rows - 1), axis=0, mod...]
    reduce_scatter x2 -> x0, waiting for transfers between devices: 301 us -> none  [the longest x1 153 us: device_step(): lax.psum_scatter(partial_rows, 'tp', scatter_dimension=0, tiled=True)]
    pallas_call x0 -> x2, Pallas kernels: none -> 218 us  [the longest x1 168 us: device_step(): pl.pallas_call(functools.partial(block_kernel, chips), out_shape=jax.Shap...]
    all_gather x1 -> x0, waiting for transfers between devices: 72 us -> none  [device_step(): normed_all = lax.all_gather(normed, 'tp', axis=0, tiled=True)]
    dot_general x1 -> x0, matrix products: 28.8 us -> none  [device_step(): jnp.dot(activated, w_out_shard, preferred_element_type=jnp.float32)]
    select_n x1, other arithmetic: 14.7 us -> 0.77 us  [device_step(): send_idx = jnp.where((local >= 0) & (local < shard_rows), local, -1)]
  transfers between devices with their start and end apart: 3 -> 0, of which waited for: 3 -> 0; matrix products, arithmetic and copies ran while one was open for 0% -> 0% of each run, Pallas kernels for 0% -> 0%
where the time goes in v1:
time: 227 us
  Pallas kernels  218 us (96%)
  local copies, waits for them, and re-layouts  6.5 us (3%)
    pallas_call x1, Pallas kernels, device_step(): pl.pallas_call(functools.partial(block_kernel, chips), out_shape=jax.Shap...  168 us
    pallas_call x1, Pallas kernels, gather_rows(): pl.pallas_call(functools.partial(gather_kernel, chunks, groups), out_shap...  50.8 us
    unnamed x2, local copies, waits for them, and re-layouts  5.23 us

profile of v1, /device:TPU:112, one launch (start us, length us, event | category | flops | bytes accessed | tf_op | source)
XLA Modules:
  0.0 227.1 jit_solution(3682814931092575089)
XLA Ops:
  0.0 1.3 fusion.4.ridx
  1.3 1.3 reshape.11.gain_ref
  2.6 0.8 and_select_fusion.idx_ref
  3.3 2.4 %copy.6.w1_hbm = bf16[896,608]{1,0:T(8,128)(2,1)} copy(bf16[896,608]{0,1:T(8,128)(2,1)} %param.8) | data formatting | bytes 2179072 | tf_op args[3]
  5.7 50.8 %shard_map.55 = bf16[1024,8,896]{2,1,0:T(8,128)(2,1)} custom-call(s32[8192]{0:T(1024)S(1)} %and_select_fusion.idx_ref, bf16[2374,8,896]{2,1,0:T(8,128)(2,1)} %bitcast.3), custom_call_target="tpu_custom_call" | custom-call | tf_op jit(solution)/shard_map/pallas_call | solution.py:58
  56.5 167.7 %shard_map.56 = bf16[1024,896]{1,0:T(8,128)(2,1)} custom-call(s32[1024]{0:T(1024)} %fusion.4.ridx, bf16[8,128,8,896]{3,2,1,0:T(8,128)(2,1)} %bitcast.2, bf16[1,896]{1,0:T(2,128)(2,1)} %reshape.11.gain_ref, bf16[896,608]{1,0:T(8,128)(2,1)} %copy.6.w1_hbm, bf16[608,896]{1,0:T(8,128)(2,1)} %w2_hbm.1), custom_call_target="tpu_custom_call" | custom-call | tf_op jit(solution)/shard_map/pallas_call | solution.py:272
  224.2 2.9 %copy.8 = bf16[1024,896]{1,0:T(8,128)(2,1)} copy(bf16[1024,896]{1,0:T(8,128)(2,1)} %shard_map.56) | data formatting | bytes 3670016
